TPU v7x, 512 devices: a whole 4x4x16 slice. The times are simulated.
512 devices in a mesh: aux: 32 (over y, x, core), shell: 16 (over z).
Axes of the slice: x: 4, y: 4, z: 16, core: 2. Of those that a mesh axis runs over, the one named last changes fastest.
Arguments:
- density: bfloat16 [128, 120, 8192], P('aux', None, 'shell'), may hold values from -6 to 6
- occ_density: bfloat16 [128, 120, 120], P('aux'), may hold values from -6 to 6
- cabs_coeff: bfloat16 [2048, 8192], P('aux', 'shell'), may hold values from -0.0625 to 0.0625
- occ_coeff: bfloat16 [2048, 120], P('aux'), may hold values from -0.5 to 0.5
- tile_owner: int32 [64, 1], replicated, may hold values from 0 to 15; in each aligned block of 64 rows (0 to 63, 64 to 127, ...) at most 8 rows name the same one
Outputs:
- ao_density: bfloat16 [128, 128, 32, 2048], P('shell', 'aux')
Inputs may be any that keep to these rules, and one draw needn't show every extreme that they name: `tile_owner`: no owner holds more than 8 blocks, and some owner holds exactly 8; every owner holds at least one block.
All inputs are finite; a program needn't handle non-finite values.
Results may differ from a plain program's by a relative error of at most 0.015.
Values may be sent and summed in bfloat16 or wider, within the bound.
A program may use at most 64 MiB of HBM per device.

v0:
```python
import jax
import jax.numpy as jnp
from jax import lax
from jax.sharding import Mesh
from jax.sharding import PartitionSpec as P

NOCC = 120
CAPT = 8
AUX = ("aux_0", "aux_1", "aux_2")


def in_order(blocks, dim):
    lengths = list(blocks.shape[1:])
    lengths[dim] *= blocks.shape[0]
    return jnp.moveaxis(blocks, 0, dim).reshape(lengths)


def gather_in_order(value, axes, sequence):
    blocks = value[None]
    for k in sequence:
        blocks = lax.all_gather(blocks, axes[k], axis=0, tiled=True)
    current = [lax.axis_size(axes[k]) for k in reversed(sequence)]
    blocks = blocks.reshape(*current, *value.shape)
    turned = sorted(range(len(sequence)), key=lambda place: sequence[len(sequence) - 1 - place])
    return blocks.transpose(*turned, *range(len(sequence), blocks.ndim)).reshape(-1, *value.shape)


def gather_axes(value, axes, sequence, dim):
    return in_order(gather_in_order(value, axes, sequence), dim)


def from_everyone(value, axis):
    copies = jnp.broadcast_to(value, (lax.axis_size(axis), *value.shape))
    return lax.all_to_all(copies, axis, split_axis=0, concat_axis=0, tiled=True)


def gather_directly(value, axis, dim):
    blocks = from_everyone(value, axis)
    return in_order(blocks, dim)


def per_device(density, occ_density, cabs_coeff, occ_coeff, tile_owner):
    local_q = density.shape[0]
    me_shell = lax.axis_index("shell")
    occ_full = gather_axes(occ_coeff, (("aux_0", "aux_1"), "aux_2"), (0, 1), 0)
    nao = occ_full.shape[0]
    ntile = tile_owner.shape[0]
    width = nao // ntile
    owned = (tile_owner[:, 0] == me_shell).astype(jnp.int32)
    rank = jnp.cumsum(owned) - 1
    select = (
        (rank[None, :] == jnp.arange(CAPT, dtype=jnp.int32)[:, None]) & (owned[None, :] == 1)
    ).astype(jnp.bfloat16)
    batches = 1
    span = local_q // batches
    flat = density.reshape(span * NOCC, density.shape[2])
    terms = lax.dot_general(
        flat,
        gather_directly(cabs_coeff, AUX, 0),
        (((1,), (1,)), ((), ())),
        preferred_element_type=jnp.float32,
    )
    summed = lax.psum(terms.astype(jnp.bfloat16), "shell").astype(jnp.float32)
    occ_term = jnp.einsum("qij,nj->qin", occ_density, occ_full, preferred_element_type=jnp.float32)
    rounded = (summed + occ_term.reshape(span * NOCC, nao)).astype(jnp.bfloat16)
    blocks = rounded.reshape(span, NOCC, ntile, width)
    half_owned = jnp.einsum(
        "kt,qitw->kqiw", select, blocks, preferred_element_type=jnp.float32
    ).astype(jnp.bfloat16)
    gamma = jnp.einsum("kqiw,mi->kqwm", half_owned, occ_full, preferred_element_type=jnp.float32)
    results = gamma.astype(jnp.bfloat16)
    return results


def solution(mesh):
    split = Mesh(
        mesh.devices.reshape(4, 4, 2, mesh.shape["shell"]), ("aux_0", "aux_1", "aux_2", "shell")
    )
    placed = (P(AUX, None, "shell"), P(AUX, None, None), P(AUX, "shell"), P(AUX, None), P())
    return jax.shard_map(
        per_device,
        mesh=split,
        in_specs=placed,
        out_specs=P("shell", AUX, None, None),
        check_vma=False,
    )
```

profile of v0, /device:TPU:2, one launch (start us, length us, event | category | flops | bytes accessed | tf_op | source)
XLA Modules:
  0.0 210.7 jit_solution(16812223826176570865)
XLA Ops:
  6.5 0.0 copy-start
  6.5 0.0 all-reduce.2.cloned.1.call-start
  6.5 1.1 broadcast_in_dim.4
  7.7 35.9 %all_to_all.5 = bf16[32,64,512]{2,1,0:T(8,128)(2,1)S(1)} all-to-all(bf16[32,64,512]{2,1,0:T(8,128)(2,1)S(1)} %broadcast_in_dim.4), channel_id=1, replica_groups=mesh['aux_0'=4,'aux_1'=4,'aux_2'=2,'shell'=16] {'aux_0','aux_1','aux_2'}, dimensions={0} | all-to-all | bytes 4194304 | tf_op jit(solution)/shard_map/all_to_all | solution.py:34
  43.6 0.0 copy-done
  43.6 0.0 copy-start.3
  43.6 0.0 copy-start.2
  43.6 2.5 %convolution_convert_fusion.1 = bf16[480,2048]{1,0:T(8,128)(2,1)} fusion(bf16[480,512]{1,0:T(8,128)(2,1)S(1)} %bitcast.24, bf16[2048,512]{1,0:T(8,128)(2,1)S(1)} %bitcast.27), kind=kOutput, calls=%fused_computation.2 | convolution fusion | flops 1007616000 | bytes 4554752 | tf_op jit(solution)/shard_map/dot_general | solution.py:57
  46.1 0.0 copy-start.1
  46.1 0.0 all-reduce.2.cloned.1.call-update
  46.1 0.0 copy-done.3
  46.2 0.1 copy.11
  46.3 0.0 copy-done.2
  46.3 22.1 %all-gather = bf16[1024,120]{1,0:T(8,128)(2,1)S(1)} all-gather(bf16[64,120]{1,0:T(8,128)(2,1)S(1)} %copy-done.2), channel_id=2, replica_groups=mesh['aux_0'=4,'aux_1'=4,'aux_2'=2,'shell'=16] {'aux_0','aux_1'}, dimensions={0}, use_global_device_ids=true | all-gather | bytes 261120 | tf_op jit(solution)/shard_map/all_gather | solution.py:21
  68.4 2.2 %all_gather.7 = bf16[32,64,120]{2,1,0:T(8,128)(2,1)S(1)} all-gather(bf16[16,64,120]{2,1,0:T(8,128)(2,1)S(1)} %bitcast.29), channel_id=1, replica_groups=mesh['aux_0'=4,'aux_1'=4,'aux_2'=2,'shell'=16] {'aux_2'}, dimensions={0}, use_global_device_ids=true | all-gather | bytes 737280 | tf_op jit(solution)/shard_map/all_gather | solution.py:21
  70.6 0.1 reduce-window.8
  70.7 0.1 add_reduce_fusion
  70.8 119.6 %all-reduce.2.cloned.1.call-done = bf16[480,2048]{1,0:T(8,128)(2,1)} async-done(((bf16[480,2048]{1,0:T(8,128)(2,1)}), bf16[480,2048]{1,0:T(8,128)(2,1)}) %all-reduce.2.cloned.1.call-update) | async-done | bytes 1966096 | tf_op jit(solution)/shard_map/psum | solution.py:63
  190.4 0.0 copy-done.1
  190.4 2.2 %add_convert_fusion = bf16[480,2048]{1,0:T(8,128)(2,1)S(1)} fusion(bf16[480,2048]{1,0:T(8,128)(2,1)} %all-reduce.2.cloned.1.call-done, bf16[480,120]{1,0:T(8,128)(2,1)S(1)} %bitcast.30, bf16[2048,120]{1,0:T(8,128)(2,1)S(1)} %bitcast.25), kind=kOutput, calls=%fused_computation | convolution fusion | flops 238878720 | bytes 4538880 | tf_op jit(solution)/shard_map/qij,nj->qin/dot_general | solution.py:64
  192.7 2.4 %copy.13 = bf16[480,2048]{0,1:T(8,128)(2,1)} copy(bf16[480,2048]{1,0:T(8,128)(2,1)S(1)} %add_convert_fusion) | data formatting | bytes 3932160 | tf_op jit(solution)/shard_map/convert_element_type | solution.py:65
  195.1 3.2 %reshape.52 = bf16[4,120,64,32]{1,0,3,2:T(4,128)(2,1)S(1)} reshape(bf16[480,2048]{0,1:T(8,128)(2,1)} %copy.13) | data formatting | bytes 3932160 | tf_op jit(solution)/shard_map/reshape | solution.py:66
  198.3 2.3 %fusion.2 = bf16[8,4,120,32]{2,0,3,1:T(8,128)(2,1)S(1)} fusion(bf16[4,120,64,32]{1,0,3,2:T(4,128)(2,1)S(1)} %reshape.52, s32[64]{0:T(128)S(1)} %add_reduce_fusion, pred[64]{0:T(512)(128)(4,1)S(1)} %get-tuple-element.5), kind=kOutput, calls=%fused_computation.5 | convolution fusion | flops 15852544 | bytes 2212160 | tf_op jit(solution)/shard_map/kt,qitw->kqiw/dot_general | solution.py:67
  200.6 3.3 %convolution_convert_fusion = bf16[8,4,32,2048]{3,2,1,0:T(8,128)(2,1)} fusion(bf16[2048,120,1,1]{1,0,3,2:T(8,128)(2,1)S(1)} %bitcast.26, bf16[8,4,120,32]{2,0,3,1:T(8,128)(2,1)S(1)} %fusion.2), kind=kOutput, calls=%fused_computation.1 | convolution fusion | flops 505413632 | bytes 4931584 | tf_op jit(solution)/shard_map/kqiw,mi->kqwm/dot_general | solution.py:70
  (2 shorter events, 0.0 us)
Async XLA Ops:
  6.5 37.0 %copy-start = (bf16[4,120,512]{2,1,0:T(8,128)(2,1)S(1)}, bf16[4,120,512]{2,1,0:T(8,128)(2,1)}, u32[]{:S(2)}) copy-start(bf16[4,120,512]{2,1,0:T(8,128)(2,1)} %param.5) | copy-start | bytes 1474564
  6.5 183.9 %all-reduce.2.cloned.1.call-start = ((), (), s32[]{:S(2)}) async-start(), calls=%async_computation.1 | async-start | bytes 3932160 | tf_op jit(solution)/shard_map/psum | solution.py:63
  43.6 2.6 %copy-start.3 = (s32[64,1]{0,1:T(1,128)S(1)}, s32[64,1]{0,1:T(1,128)}, u32[]{:S(2)}) copy-start(s32[64,1]{0,1:T(1,128)} %param.9) | copy-start | bytes 772
  43.6 2.7 %copy-start.2 = (bf16[64,120]{1,0:T(8,128)(2,1)S(1)}, bf16[64,120]{1,0:T(8,128)(2,1)}, u32[]{:S(2)}) copy-start(bf16[64,120]{1,0:T(8,128)(2,1)} %param.8) | copy-start | bytes 46084
  46.1 144.3 %copy-start.1 = (bf16[4,120,120]{2,1,0:T(8,128)(2,1)S(1)}, bf16[4,120,120]{2,1,0:T(8,128)(2,1)}, u32[]{:S(2)}) copy-start(bf16[4,120,120]{2,1,0:T(8,128)(2,1)} %param.6) | copy-start | bytes 345604
Sparse Core Ops, SparseCore 0:
  46.3 144.1 all-reduce.1
where the time goes:
time: 211 us
  waiting for transfers between devices  120 us (57%)
  blocking collectives  60.2 us (29%)
  between operations  13.5 us (6%)
  matrix products  10.3 us (5%)
  local copies, waits for them, and re-layouts  6.88 us (3%)
    psum x1, waiting for transfers between devices, per_device(): summed = lax.psum(terms.astype(jnp.bfloat16), 'shell').astype(jnp.float32)  120 us
    all_to_all x1, blocking collectives, from_everyone(): return lax.all_to_all(copies, axis, split_axis=0, concat_axis=0, tiled=True)  35.9 us
    all_gather x2, blocking collectives, gather_in_order(): blocks = lax.all_gather(blocks, axes[k], axis=0, tiled=True)  24.3 us
  transfers between devices with their start and end apart: 1, of which 1 were waited for; matrix products, arithmetic and copies ran while one was open for 0% of the time, Pallas kernels for 0%

commit v1 on v0

v1 whole, which is shorter than its diff:
```python
import jax
import jax.numpy as jnp
from jax import lax
from jax.experimental import pallas as pl
from jax.experimental.pallas import tpu as pltpu
from jax.sharding import Mesh
from jax.sharding import PartitionSpec as P

AXES = ("y", "x", "c")
OFFSETS = (1, 3, 2)
ORDER = (0, 1, 3, 2)
NOCC, ZN, SLOTS, BW, TILES = 120, 16, 8, 32, 64
NQ, NG, GW, ST = 4, 4, 8, 4
LANES = 128
FAR = (8, 7, 9, 6, 10, 5, 11, 4, 12, 3, 13, 2, 14, 1, 15)
F32, BF16 = jnp.float32, jnp.bfloat16


def nt(a, b):
    return lax.dot_general(a, b, (((1,), (1,)), ((), ())), preferred_element_type=F32)


def exchange(
    dens, occd, cabs, occ, own_row, own_col, half_out, occ_out,
    xv, dv, cv, ga, gb, og, part, recv, send, sel, oterm, orow, asend, arecv,
    lsem, gs, gr, rs, rr, ts, tr,
):
    y, x, c, z = (lax.axis_index(a) for a in ("y", "x", "c", "z"))
    size = {"y": 4, "x": 4, "c": 2, "z": ZN}

    def at(axis, offset):
        return {axis: lax.rem(lax.axis_index(axis) + offset % size[axis], size[axis])}

    loads = [
        pltpu.make_async_copy(cabs, cv, lsem.at[0]),
        pltpu.make_async_copy(dens, xv, lsem.at[1]),
        pltpu.make_async_copy(occ, og.at[y, x, c], lsem.at[2]),
        pltpu.make_async_copy(occd, dv, lsem.at[3]),
    ]
    for load in loads:
        load.start()
    barrier = pltpu.get_barrier_semaphore()
    peers = [at(a, o) for a in ("x", "y") for o in OFFSETS] + [at("c", 1), at("z", 1), at("z", -1)]
    for peer in peers:
        pl.semaphore_signal(barrier, inc=1, device_id=peer, device_id_type=pl.DeviceIdType.MESH)

    count = [0]
    started = []

    def copy(src, dst, peer):
        k = count[0]
        count[0] += 1
        made = pltpu.make_async_remote_copy(
            src_ref=src, dst_ref=dst, send_sem=gs.at[k], recv_sem=gr.at[k],
            device_id=peer, device_id_type=pl.DeviceIdType.MESH,
        )
        made.start()
        started.append(made)
        return made

    loads[0].wait()
    mine = cv[...].astype(F32).reshape(2, NG, GW, cv.shape[1])
    ra = pl.multiple_of(c * 64 + x * 16, 16)
    rb = pl.multiple_of(c * 64 + y * 16, 16)
    for g in range(2):
        ga[y, g, pl.ds(ra, 16), :] = jnp.concatenate([mine[0, g], mine[1, g]], 0).astype(BF16)
        gb[x, g, pl.ds(rb, 16), :] = jnp.concatenate([mine[0, g + 2], mine[1, g + 2]], 0).astype(BF16)
    pl.semaphore_wait(barrier, len(peers))

    def blk_a(o):
        r = pl.multiple_of(c * 64 + lax.rem(x + 4 - o, 4) * 16, 16)
        return ga.at[y, :, pl.ds(r, 16), :]

    def blk_b(o):
        r = pl.multiple_of(c * 64 + lax.rem(y + 4 - o, 4) * 16, 16)
        return gb.at[x, :, pl.ds(r, 16), :]

    rc = pl.multiple_of(c * 64, 64)

    def qtr_a(o):
        return ga.at[lax.rem(y + 4 - o, 4), :, pl.ds(rc, 64), :]

    def qtr_b(o):
        return gb.at[lax.rem(x + 4 - o, 4), :, pl.ds(rc, 64), :]

    other = at("c", 1)
    a1 = [copy(blk_a(0), blk_a(0), at("x", o)) for o in OFFSETS]
    b1 = [copy(blk_b(0), blk_b(0), at("y", o)) for o in OFFSETS]
    fwd0 = [copy(blk_a(0), blk_a(0), other), copy(blk_b(0), blk_b(0), other)]
    for i, o in enumerate(OFFSETS):
        a1[i].wait_recv()
        fwd0.append(copy(blk_a(o), blk_a(o), other))
    a2 = [copy(qtr_a(0), qtr_a(0), at("y", o)) for o in OFFSETS]
    for i, o in enumerate(OFFSETS):
        b1[i].wait_recv()
        fwd0.append(copy(blk_b(o), blk_b(o), other))
    b2 = [copy(qtr_b(0), qtr_b(0), at("x", o)) for o in OFFSETS]
    loads[2].wait()
    o1 = [copy(og.at[y, x, c], og.at[y, x, c], at("x", o)) for o in OFFSETS]
    loads[1].wait()
    loads[3].wait()

    fwd = {}

    def forward(j):
        a2[j - 1].wait_recv()
        b2[j - 1].wait_recv()
        fwd[j] = (copy(qtr_a(ORDER[j]), qtr_a(ORDER[j]), other), copy(qtr_b(ORDER[j]), qtr_b(ORDER[j]), other))

    def compute(j):
        for made in fwd0 if j == 0 else fwd[j]:
            made.wait_recv()
        for base, ref in ((0, ga.at[lax.rem(y + 4 - ORDER[j], 4)]), (2, gb.at[lax.rem(x + 4 - ORDER[j], 4)])):
            got = nt(xv[...], ref[...].reshape(2 * LANES, xv.shape[1]))
            for q in range(NQ):
                for g in range(2):
                    part[j, q * NG + base + g] = got[q * NOCC:(q + 1) * NOCC, g * LANES:(g + 1) * LANES]

    def ring(way, s, j):
        return pltpu.make_async_remote_copy(
            src_ref=send.at[way, s, j], dst_ref=recv.at[way, s, j], send_sem=rs.at[way, s, j],
            recv_sem=rr.at[way, s, j], device_id=at("z", 1 if way == 0 else -1), device_id_type=pl.DeviceIdType.MESH,
        )

    def travels(way, s, j):
        return s >= 1 or way == j % 2

    def step(j, s):
        for way in range(2):
            if not travels(way, s, j):
                continue
            dest = lax.rem(z + (8 - s if way == 0 else 8 + s), ZN)
            value = part[j, dest]
            if s >= 1 and travels(way, s - 1, j):
                ring(way, s - 1, j).wait_recv()
                value = value + recv[way, s - 1, j].astype(F32)
            send[way, s, j] = value.astype(BF16)
            ring(way, s, j).start()

    q_me, g_me = z // NG, lax.rem(z, NG)

    def tile_of(stream, core, v, low):
        o = jnp.where(stream == 0, 0, jnp.where(stream == 1, 1, jnp.where(stream == 2, 3, 2)))
        ta = ((y + 4 - o) & 3) * 16 + v * 4
        tb = v * 16 + ((x + 4 - o) & 3) * 4
        return jnp.where(g_me < 2, ta, tb) + core * 2 + low

    def selection():
        row, col = own_row[...], own_col[...]
        before = lax.broadcasted_iota(jnp.int32, (TILES, TILES), 0) < lax.broadcasted_iota(jnp.int32, (TILES, TILES), 1)
        rank = jnp.sum(jnp.where(before & (col == row), 1.0, 0.0), axis=0, keepdims=True)
        slot = (row * SLOTS).astype(F32) + rank
        lane = lax.broadcasted_iota(jnp.int32, (TILES, ST * LANES), 1)
        tile = tile_of(lane >> 7, (lane >> 6) & 1, (lane >> 4) & 3, (lane >> 3) & 1)
        spread = jnp.where(tile == lax.broadcasted_iota(jnp.int32, (TILES, ST * LANES), 0), 1.0, 0.0).astype(BF16)
        lifted = lax.dot_general(
            jnp.broadcast_to(slot, (8, TILES)).astype(BF16), spread, (((1,), (0,)), ((), ())), preferred_element_type=F32
        )
        place = lifted[0:1].astype(jnp.int32) * GW + (lax.broadcasted_iota(jnp.int32, (1, ST * LANES), 1) & 7)
        for o in range(ZN):
            rows = lax.broadcasted_iota(jnp.int32, (64, ST * LANES), 0) + o * 64
            sel[o * 64:(o + 1) * 64, :] = jnp.where(rows == place, 1.0, 0.0).astype(BF16)

    fo, o2 = [], []

    def occ_second():
        for made in o1:
            made.wait_recv()
        o2.extend(copy(og.at[y, :, c], og.at[y, :, c], at("y", o)) for o in OFFSETS)
        fo.append(copy(og.at[y, :, c], og.at[y, :, c], other))

    def occ_third():
        for i, o in enumerate(OFFSETS):
            o2[i].wait_recv()
            yy = lax.rem(y + 4 - o, 4)
            fo.append(copy(og.at[yy, :, c], og.at[yy, :, c], other))

    def occ_last():
        for made in fo:
            made.wait_recv()
        occ_out[...] = og[...]

    def occ_term():
        for j in range(ST):
            for r in range(16):
                core, v, low = r // 8, (r // 2) % 4, r % 2
                t = tile_of(j, core, v, low)
                got = og[t // 16, (t // 4) & 3, core, low * NG + g_me]
                orow[(j * 16 + r) * GW:(j * 16 + r + 1) * GW, :] = got.astype(F32)
        oterm[...] = nt(dv[q_me], orow[...].astype(BF16))

    compute(0)
    step(0, 0)
    step(0, 1)
    forward(1)
    forward(2)
    compute(1)
    step(1, 0)
    compute(2)
    step(2, 0)
    step(0, 2)
    forward(3)
    step(1, 1)
    step(2, 1)
    step(0, 3)
    compute(3)
    step(3, 0)
    occ_second()
    at_step = [4, 2, 2, 1]
    side = [selection, occ_third, occ_last, occ_term]
    while min(at_step) < 8:
        for j in range(ST):
            if at_step[j] < 8:
                step(j, at_step[j])
                at_step[j] += 1
        if side:
            side.pop(0)()

    total = []
    for j in range(ST):
        value = part[j, z] + oterm[:, j * LANES:(j + 1) * LANES]
        for way in range(2):
            ring(way, 7, j).wait_recv()
            value = value + recv[way, 7, j].astype(F32)
        total.append(value.astype(BF16))
    half = jnp.concatenate(total, axis=1)
    picked = lax.dot_general(sel[...], half, (((1,), (1,)), ((), ())), preferred_element_type=F32)
    asend[...] = picked.reshape(ZN, SLOTS, GW, NOCC).astype(BF16)

    def route(k):
        to = lax.rem(z + k, ZN)
        return pltpu.make_async_remote_copy(
            src_ref=asend.at[to], dst_ref=arecv.at[z], send_sem=ts.at[k], recv_sem=tr.at[k],
            device_id={"z": to}, device_id_type=pl.DeviceIdType.MESH,
        )

    for k in FAR:
        route(k).start()
    arecv[z] = asend[z]
    for made in started:
        made.wait_send()
    for way in range(2):
        for s in range(8):
            for j in range(ST):
                if travels(way, s, j):
                    ring(way, s, j).wait_send()
    for k in FAR:
        route(k).wait_recv()
    half_out[...] = arecv[...]
    for k in FAR:
        route(k).wait_send()


def final(half, occ, out):
    rows = half[...].astype(F32)
    kk = rows.shape[1]
    lhs = jnp.concatenate([rows[:, k].reshape(LANES, NOCC) for k in range(kk)], axis=0).astype(BF16)
    got = nt(lhs, occ[...])
    out[...] = got.reshape(kk, NQ, BW, got.shape[1]).astype(BF16)


def per_device(density, occ_density, cabs_coeff, occ_coeff, tile_owner):
    nq, nocc, ncab = density.shape
    rows = nq * nocc
    nao = TILES * BW
    any_spec = pl.BlockSpec(memory_space=pl.ANY)
    vmem = pl.BlockSpec(memory_space=pltpu.VMEM)
    half, occ_full = pl.pallas_call(
        exchange,
        out_shape=(
            jax.ShapeDtypeStruct((ZN, SLOTS, GW, nocc), BF16),
            jax.ShapeDtypeStruct((4, 4, 2, 8, GW, nocc), BF16),
        ),
        in_specs=[any_spec] * 4 + [vmem] * 2,
        out_specs=(vmem, vmem),
        scratch_shapes=[
            pltpu.VMEM((rows, ncab), BF16),
            pltpu.VMEM((nq, nocc, nocc), BF16),
            pltpu.VMEM((64, ncab), BF16),
            pltpu.VMEM((4, 2, LANES, ncab), BF16),
            pltpu.VMEM((4, 2, LANES, ncab), BF16),
            pltpu.VMEM((4, 4, 2, 8, GW, nocc), BF16),
            pltpu.VMEM((ST, ZN, nocc, LANES), F32),
            pltpu.VMEM((2, 8, ST, nocc, LANES), BF16),
            pltpu.VMEM((2, 8, ST, nocc, LANES), BF16),
            pltpu.VMEM((ZN * SLOTS * GW, ST * LANES), BF16),
            pltpu.VMEM((nocc, ST * LANES), F32),
            pltpu.VMEM((ST * LANES, nocc), F32),
            pltpu.VMEM((ZN, SLOTS, GW, nocc), BF16),
            pltpu.VMEM((ZN, SLOTS, GW, nocc), BF16),
            pltpu.SemaphoreType.DMA((4,)),
            pltpu.SemaphoreType.DMA((36,)),
            pltpu.SemaphoreType.DMA((36,)),
            pltpu.SemaphoreType.DMA((2, 8, ST)),
            pltpu.SemaphoreType.DMA((2, 8, ST)),
            pltpu.SemaphoreType.DMA((ZN,)),
            pltpu.SemaphoreType.DMA((ZN,)),
        ],
        compiler_params=pltpu.CompilerParams(
            collective_id=0, has_side_effects=True, vmem_limit_bytes=40 * 1024 * 1024
        ),
    )(
        density.reshape(rows, ncab),
        occ_density,
        cabs_coeff,
        occ_coeff.reshape(8, GW, nocc),
        tile_owner.reshape(1, TILES),
        tile_owner,
    )
    steps = 4
    per = SLOTS // steps
    return pl.pallas_call(
        final,
        grid=(steps,),
        out_shape=jax.ShapeDtypeStruct((SLOTS, nq, BW, nao), BF16),
        in_specs=[
            pl.BlockSpec((ZN, per, GW, nocc), lambda k: (0, k, 0, 0)),
            pl.BlockSpec((nao, nocc), lambda k: (0, 0)),
        ],
        out_specs=pl.BlockSpec((per, nq, BW, nao), lambda k: (k, 0, 0, 0)),
    )(half, occ_full.reshape(nao, nocc))


def solution(mesh):
    split = Mesh(mesh.devices.reshape(4, 4, 2, mesh.shape["shell"]), (*AXES, "z"))
    placed = (P(AXES, None, "z"), P(AXES, None, None), P(AXES, "z"), P(AXES, None), P())
    return jax.shard_map(
        per_device, mesh=split, in_specs=placed, out_specs=P("z", AXES, None, None), check_vma=False
    )
```

time: 211 us -> 83.6 us (0.40)
  the two profiles are of different devices: /device:TPU:2 before, /device:TPU:32 now
where the time goes in v1:
time: 83.6 us; the launch traced here: 83.2 us
  Pallas kernels  76.8 us (92%)
  local copies, waits for them, and re-layouts  6.36 us (8%)
    pallas_call x1, Pallas kernels, per_device(): pl.pallas_call(exchange, out_shape=(jax.ShapeDtypeStruct((ZN, SLOTS, GW,...  72 us
    unnamed x15, local copies, waits for them, and re-layouts  6.36 us
    pallas_call x1, Pallas kernels, per_device(): pl.pallas_call(final, grid=(steps,), out_shape=jax.ShapeDtypeStruct((SLOT...  4.74 us

profile of v1, /device:TPU:32, one launch (start us, length us, event | category | flops | bytes accessed | tf_op | source)
XLA Modules:
  0.0 83.2 jit_solution(3155156788445467390)
XLA Ops:
  0.0 0.7 copy.6.own_col
  0.7 0.0 copy-start.1
  0.7 1.0 %copy-done.1 = bf16[4,120,512]{2,1,0:T(8,128)(2,1)S(1)} copy-done((bf16[4,120,512]{2,1,0:T(8,128)(2,1)S(1)}, bf16[4,120,512]{2,1,0:T(8,128)(2,1)}, u32[]{:S(2)}) %copy-start.1) | copy-done | bytes 491544
  1.8 0.0 copy-start.3
  1.8 0.9 %copy-done.3 = bf16[4,120,120]{2,1,0:T(8,128)(2,1)S(1)} copy-done((bf16[4,120,120]{2,1,0:T(8,128)(2,1)S(1)}, bf16[4,120,120]{2,1,0:T(8,128)(2,1)}, u32[]{:S(2)}) %copy-start.3) | copy-done | bytes 115224
  2.7 0.0 copy-start.4
  2.7 0.8 %copy-done.4 = bf16[64,512]{1,0:T(8,128)(2,1)S(1)} copy-done((bf16[64,512]{1,0:T(8,128)(2,1)S(1)}, bf16[64,512]{1,0:T(8,128)(2,1)}, u32[]{:S(2)}) %copy-start.4) | copy-done | bytes 65560
  3.5 0.0 copy-start.5
  3.5 0.7 copy-done.5
  4.2 0.0 copy-start.6
  4.2 0.7 copy-done.6
  4.9 72.0 %shard_map.55 = (bf16[16,8,8,120]{3,2,1,0:T(8,128)(2,1)S(1)}, bf16[4,4,2,8,8,120]{5,4,3,2,1,0:T(8,128)(2,1)S(1)}) custom-call(bf16[480,512]{1,0:T(8,128)(2,1)S(1)} %bitcast.5, bf16[4,120,120]{2,1,0:T(8,128)(2,1)S(1)} %copy-done.3, bf16[64,512]{1,0:T(8,128)(2,1)S(1)} %copy-done.4, bf16[8,8,120]{2,1,0:T(8,128)(2,1)S(1)} %bitcast.6, s32[1,64]{1,0:T(1,128)S(1)} %bitcast.7, ...), custom_call_target="tpu_custom_call" | custom-call | tf_op jit(solution)/shard_map/pallas_call | solution.py:268
  76.9 0.0 copy-start
  77.0 0.8 copy-done
  77.7 0.0 copy-start.2
  77.7 0.7 copy-done.2
  78.4 4.7 %shard_map.56 = bf16[8,4,32,2048]{3,2,1,0:T(8,128)(2,1)} custom-call(bf16[16,8,8,120]{3,2,1,0:T(8,128)(2,1)} %copy-done.2, bf16[2048,120]{1,0:T(8,128)(2,1)} %bitcast.4), custom_call_target="tpu_custom_call" | custom-call | tf_op jit(solution)/shard_map/pallas_call | solution.py:312
Async XLA Ops:
  0.7 1.0 %copy-start.1 = (bf16[4,120,512]{2,1,0:T(8,128)(2,1)S(1)}, bf16[4,120,512]{2,1,0:T(8,128)(2,1)}, u32[]{:S(2)}) copy-start(bf16[4,120,512]{2,1,0:T(8,128)(2,1)} %param.5) | copy-start | bytes 1474564
  1.8 0.9 %copy-start.3 = (bf16[4,120,120]{2,1,0:T(8,128)(2,1)S(1)}, bf16[4,120,120]{2,1,0:T(8,128)(2,1)}, u32[]{:S(2)}) copy-start(bf16[4,120,120]{2,1,0:T(8,128)(2,1)} %occd.1) | copy-start | bytes 345604
  2.7 0.8 %copy-start.4 = (bf16[64,512]{1,0:T(8,128)(2,1)S(1)}, bf16[64,512]{1,0:T(8,128)(2,1)}, u32[]{:S(2)}) copy-start(bf16[64,512]{1,0:T(8,128)(2,1)} %cabs.1) | copy-start | bytes 196612
  3.5 0.7 copy-start.5
  4.2 0.7 copy-start.6
  76.9 0.8 copy-start
  77.7 0.7 copy-start.2
